TPU v7x, 32 devices: a whole 2x2x4 slice. The times are simulated.
32 devices in a mesh: pipe: 4 (over y, core), tensor: 8 (over z, x).
Axes of the slice: x: 2, y: 2, z: 4, core: 2. Of those that a mesh axis runs over, the one named last changes fastest.
Arguments:
- patches: bfloat16 [16384, 1280], P(('pipe', 'tensor')), may hold values from -6 to 6
- attn_gain: float32 [1280], replicated, may hold values from 0.25 to 1.75
- w_qkv: bfloat16 [1280, 3840], P('tensor', 'pipe'), may hold values from -0.1118034 to 0.1118034
- w_out: bfloat16 [1280, 1280], P('tensor', 'pipe'), may hold values from -0.15625 to 0.15625
- merge_gain: float32 [1280], replicated, may hold values from 0.25 to 1.75
- window_ids: int32 [16384], P(('pipe', 'tensor')), may hold values from 0 to 127, as said below
- image_patches: int32 [128], P(('pipe', 'tensor')), may hold values from 0 to 512, as said below
- image_sample: int32 [128], P(('pipe', 'tensor')), may hold values from 0 to 7
Outputs:
- vision_seq: bfloat16 [4, 128, 8, 5120], P('pipe', None, 'tensor')
Inputs may be any that keep to these rules, and one draw needn't show every extreme that they name: `window_ids`: Non-decreasing within each bundle and equal over each 4 consecutive slots; every window lies within one aligned block of 64 slots of a bundle. `image_patches`: multiples of 128; the images of one bundle take at most 512 slots and at least half of them, and in every micro-batch some bundle is full.
All inputs are finite; a program needn't handle non-finite values.
Results may differ from a plain program's by a relative error of at most 0.0053.
Values may be sent and summed in bfloat16 or wider, within the bound.
A program may use at most 64 MiB of HBM per device.

v0:
```python
import math

import jax
import jax.numpy as jnp
from jax import lax
from jax.sharding import PartitionSpec as P

HEADS = 16
WINDOW = 64
SAMPLES = 8


epsilon = 1e-06


def normalize(values, gain_row):
    return (
        values * lax.rsqrt(jnp.mean(values * values, axis=-1, keepdims=True) + epsilon) * gain_row
    )


def token_positions(starts, merged_count, token_count):
    offsets = jnp.cumsum(merged_count) - merged_count
    token_index = jnp.arange(token_count, dtype=jnp.int32)
    inside = (token_index[None, :] >= offsets[:, None]) & (
        token_index[None, :] < (offsets + merged_count)[:, None]
    )
    position = jnp.sum(
        jnp.where(inside, starts[:, None] + token_index[None, :] - offsets[:, None], 0), axis=0
    )
    return jnp.where(jnp.any(inside, axis=0), position, -1)


def body(patches, attn_gain, w_qkv, w_out, merge_gain, window_ids, image_patches, image_sample):
    patch_count, feature_width = patches.shape
    token_count = patch_count // 4
    group_size = lax.axis_size("tensor")
    own_index = lax.axis_index("tensor")
    residual = patches.astype(jnp.float32)
    normed = normalize(residual, attn_gain).astype(jnp.bfloat16)
    qkv_rows = lax.all_gather(w_qkv, "tensor", axis=0, tiled=True)
    qkv = jnp.dot(
        normed,
        lax.all_gather(qkv_rows, "pipe", axis=1, tiled=True),
        preferred_element_type=jnp.float32,
    ).astype(jnp.bfloat16)
    head_width = feature_width // HEADS
    tile_count = patch_count // WINDOW

    def split_heads(block):
        return block.reshape(tile_count, WINDOW, HEADS, head_width)

    queries = split_heads(qkv[:, :feature_width])
    keys_tile = split_heads(qkv[:, feature_width : 2 * feature_width])
    values_tile = split_heads(qkv[:, 2 * feature_width :])
    scores = jnp.einsum(
        "tqhd,tkhd->thqk", queries, keys_tile, preferred_element_type=jnp.float32
    ) * (1.0 / math.sqrt(head_width))
    live_row = jnp.arange(patch_count, dtype=jnp.int32) < jnp.sum(image_patches)
    window_tile = window_ids.reshape(tile_count, WINDOW)
    live_tile = live_row.reshape(tile_count, WINDOW)
    allowed = (window_tile[:, :, None] == window_tile[:, None, :]) & live_tile[:, None, :]
    scores = jnp.where(allowed[:, None, :, :], scores, -1e30)
    row_max = jnp.max(scores, axis=-1, keepdims=True)
    exponent = jnp.exp(scores - row_max)
    weights = (exponent / jnp.sum(exponent, axis=-1, keepdims=True)).astype(jnp.bfloat16)
    context = jnp.einsum(
        "thqk,tkhd->tqhd", weights, values_tile, preferred_element_type=jnp.float32
    ).reshape(patch_count, feature_width)
    context = jnp.where(live_row[:, None], context, 0.0).astype(jnp.bfloat16)
    proj_rows = lax.all_gather(w_out, "tensor", axis=0, tiled=True)
    attended = jnp.dot(
        context,
        lax.all_gather(proj_rows, "pipe", axis=1, tiled=True),
        preferred_element_type=jnp.float32,
    )
    hidden = residual + attended
    merged = (
        normalize(hidden, merge_gain).astype(jnp.bfloat16).reshape(token_count, 4 * feature_width)
    )
    outgoing = merged.reshape(token_count // group_size, group_size, 4 * feature_width)
    merged_count = image_patches // 4
    sample_hot = image_sample[:, None] == jnp.arange(SAMPLES, dtype=jnp.int32)[None, :]
    sample_tally = jnp.sum(jnp.where(sample_hot, merged_count[:, None], 0), axis=0)
    all_tallies = lax.all_gather(sample_tally[None, :], "tensor", axis=0, tiled=True)
    source_ranks = jnp.arange(group_size, dtype=jnp.int32)
    before = jnp.sum(jnp.where((source_ranks < own_index)[:, None], all_tallies, 0), axis=0)
    totals = jnp.sum(all_tallies, axis=0)
    sample_index = jnp.arange(SAMPLES, dtype=jnp.int32)
    sample_base = jnp.sum(
        jnp.where(sample_index[None, :] < sample_index[:, None], totals[None, :], 0), axis=1
    )
    image_order = jnp.arange(image_sample.shape[0], dtype=jnp.int32)
    same_before = (image_sample[None, :] == image_sample[:, None]) & (
        image_order[None, :] < image_order[:, None]
    )
    earlier = jnp.sum(jnp.where(same_before, merged_count[None, :], 0), axis=1)
    starts = jnp.sum(jnp.where(sample_hot, (sample_base + before)[None, :], 0), axis=1) + earlier
    position = token_positions(starts, merged_count, token_count)
    outgoing_position = position.reshape(token_count // group_size, group_size)
    received, received_position = (
        lax.all_to_all(outgoing, "tensor", split_axis=1, concat_axis=0, tiled=True),
        lax.all_to_all(outgoing_position, "tensor", split_axis=1, concat_axis=0, tiled=True),
    )
    dest_rows = received_position.reshape(token_count) // group_size
    placement = (jnp.arange(token_count, dtype=jnp.int32)[:, None] == dest_rows[None, :]).astype(
        jnp.bfloat16
    )
    placed = jnp.dot(
        placement,
        received.reshape(token_count, 4 * feature_width),
        preferred_element_type=jnp.float32,
    )
    return placed.astype(jnp.bfloat16).reshape(1, token_count, 1, 4 * feature_width)


def solution(mesh):
    return jax.shard_map(
        body,
        mesh=mesh,
        in_specs=(
            P(("pipe", "tensor"), None),
            P(),
            P("tensor", "pipe"),
            P("tensor", "pipe"),
            P(),
            P(("pipe", "tensor")),
            P(("pipe", "tensor")),
            P(("pipe", "tensor")),
        ),
        out_specs=P("pipe", None, "tensor", None),
        check_vma=False,
    )
```

profile of v0, /device:TPU:0, one launch (start us, length us, event | category | flops | bytes accessed | tf_op | source)
XLA Modules:
  0.0 223.8 jit_solution(180956799762831658)
XLA Ops:
  6.5 0.7 all-gather.5.cloned.1.call-update
  7.3 59.4 %all-gather.5.cloned.1.call-done = bf16[1280,960]{1,0:T(8,128)(2,1)} async-done(((bf16[160,960]{1,0:T(8,128)(2,1)}), bf16[1280,960]{1,0:T(8,128)(2,1)}) %all-gather.5.cloned.1.call-update) | async-done | bytes 2457616 | tf_op jit(solution)/shard_map/all_gather | solution.py:41
  66.7 4.4 %copy.40 = bf16[1280,960]{0,1:T(8,128)(2,1)} copy(bf16[1280,960]{1,0:T(8,128)(2,1)} %all-gather.5.cloned.1.call-done) | data formatting | bytes 4915200 | tf_op jit(solution)/shard_map/all_gather | solution.py:41
  71.2 33.0 %all_gather.18 = bf16[1280,320]{1,0:T(8,128)(2,1)S(1)} all-gather(bf16[160,320]{1,0:T(8,128)(2,1)S(1)} %copy-done.3), channel_id=1, replica_groups=mesh['pipe'=4,'tensor'=8] {'tensor'}, dimensions={0}, use_global_device_ids=true | all-gather | bytes 921600 | tf_op jit(solution)/shard_map/all_gather | solution.py:71
  104.2 1.3 copy.46
  108.0 8.6 %all-reduce = s32[64]{0:T(128)S(1)} all-reduce(s32[64]{0:T(128)S(1)} %dynamic-update-slice), channel_id=2, replica_groups=mesh['pipe'=4,'tensor'=8] {'tensor'}, use_global_device_ids=true, to_apply=%add | all-reduce | flops 64 | bytes 512
  118.2 4.5 %all-to-all-start = ((s32[16,8,1]{0,2,1:T(1,128)}), s32[16,8,1]{0,2,1:T(1,128)S(1)}, u32[]{:S(2)}, u32[]{:S(2)}) async-start(s32[16,8,1]{0,2,1:T(1,128)} %copy.39), calls=%async_computation | async-start | bytes 8192 | tf_op jit(solution)/shard_map/all_to_all | solution.py:103
  124.7 11.6 %all-gather.7.cloned.1.call-done = bf16[1280,3840]{0,1:T(8,128)(2,1)} async-done(((bf16[1280,960]{0,1:T(8,128)(2,1)}), bf16[1280,3840]{0,1:T(8,128)(2,1)}) %all-gather.7.cloned.1.call-update) | async-done | bytes 9830416 | tf_op jit(solution)/shard_map/all_gather | solution.py:44
  136.3 9.5 %convolution_convert_fusion.1 = bf16[512,3840]{1,0:T(8,128)(2,1)S(1)} fusion(bf16[1280,3840]{0,1:T(8,128)(2,1)} %all-gather.7.cloned.1.call-done, bf16[512,1280]{1,0:T(8,128)(2,1)S(1)} %copy-done.1, f32[1280]{0:T(1024)S(1)} %copy-done.7, f32[512]{0:T(512)S(1)} %add_rsqrt_fusion.1), kind=kOutput, calls=%fused_computation.2 | convolution fusion | flops 5037752320 | bytes 15080448 | tf_op jit(solution)/shard_map/dot_general | solution.py:42
  145.8 1.7 fusion.26
  147.5 4.1 %reshape.158 = bf16[8,64,16,80]{3,2,1,0:T(8,128)(2,1)S(1)} reshape(bf16[512,1280]{1,0:T(8,128)(2,1)} %get-tuple-element.9) | data formatting | bytes 2621440 | tf_op jit(solution)/shard_map/reshape | solution.py:51
  151.6 5.0 %reshape.159 = bf16[8,64,16,80]{3,2,1,0:T(8,128)(2,1)} reshape(bf16[512,1280]{1,0:T(8,128)(2,1)} %get-tuple-element.8) | data formatting | bytes 2621440 | tf_op jit(solution)/shard_map/reshape | solution.py:51
  156.7 4.1 %reshape.157 = bf16[8,64,16,80]{3,2,1,0:T(8,128)(2,1)} reshape(bf16[512,1280]{1,0:T(8,128)(2,1)S(1)} %get-tuple-element.7) | data formatting | bytes 2621440 | tf_op jit(solution)/shard_map/reshape | solution.py:51
  160.8 2.8 %fusion.7 = f32[8,16,64,64]{2,3,1,0:T(8,128)S(1)} fusion(bf16[8,64,16,80]{3,2,1,0:T(8,128)(2,1)} %reshape.159, bf16[8,64,16,80]{3,2,1,0:T(8,128)(2,1)S(1)} %reshape.158), kind=kOutput, calls=%fused_computation.19 | convolution fusion | flops 83886080 | bytes 4718592 | tf_op jit(solution)/shard_map/tqhd,tkhd->thqk/dot_general | solution.py:56
  163.6 1.5 fusion.27
  165.2 1.2 convolution_bitcast_fusion
  166.4 1.4 copy.45
  167.8 3.3 %reshape.160 = bf16[512,1280]{1,0:T(8,128)(2,1)} reshape(bf16[8,64,16,80]{3,2,1,0:T(8,128)(2,1)S(1)} %copy.45) | data formatting | bytes 2621440 | tf_op jit(solution)/shard_map/reshape | solution.py:69
  171.1 4.3 %multiply_reduce_fusion = (f32[512]{0:T(512)S(1)}, f32[512,1280]{1,0:T(8,128)S(1)}) fusion(bf16[1280,1280]{0,1:T(8,128)(2,1)} %all-gather.9.cloned.1.call-done, bf16[512,1280]{1,0:T(8,128)(2,1)} %reshape.160, pred[512]{0:T(512)(128)(4,1)S(1)} %iota_compare_fusion.3, bf16[512,1280]{1,0:T(8,128)(2,1)S(1)} %copy-done.2), kind=kOutput, calls=%fused_computation.15 | convolution fusion | flops 1680997888 | bytes 8522240 | tf_op jit(solution)/shard_map/dot_general | solution.py:72
  175.7 0.8 reshape_reshape.3
  176.6 1.8 copy.47
  178.3 5.5 %all-to-all-start.1 = ((bf16[16,8,5120]{2,0,1:T(8,128)(2,1)}), bf16[16,8,5120]{2,0,1:T(8,128)(2,1)S(1)}, u32[]{:S(2)}, u32[]{:S(2)}) async-start(bf16[16,8,5120]{2,0,1:T(8,128)(2,1)} %copy.47), calls=%async_computation.1 | async-start | bytes 2621440 | tf_op jit(solution)/shard_map/all_to_all | solution.py:102
  184.0 31.7 %all-to-all-done.1 = bf16[16,8,5120]{2,0,1:T(8,128)(2,1)S(1)} async-done(((bf16[16,8,5120]{2,0,1:T(8,128)(2,1)}), bf16[16,8,5120]{2,0,1:T(8,128)(2,1)S(1)}, u32[]{:S(2)}, u32[]{:S(2)}) %all-to-all-start.1) | async-done | bytes 1310752 | tf_op jit(solution)/shard_map/all_to_all | solution.py:102
  215.7 1.6 fusion.1
  (58 shorter events, 6.0 us)
Async XLA Ops:
  6.5 60.1 %all-gather.5.cloned.1.call-start = ((), (), s32[]{:S(2)}) async-start(), calls=%async_computation.2 | async-start | bytes 2949120 | tf_op jit(solution)/shard_map/all_gather | solution.py:41
  7.3 63.9 %copy-start.3 = (bf16[160,320]{1,0:T(8,128)(2,1)S(1)}, bf16[160,320]{1,0:T(8,128)(2,1)}, u32[]{:S(2)}) copy-start(bf16[160,320]{1,0:T(8,128)(2,1)} %param.11) | copy-start | bytes 307204
  7.3 129.0 %all-gather.7.cloned.1.call-start = ((), (), s32[]{:S(2)}) async-start(), calls=%async_computation.3 | async-start | bytes 12288000 | tf_op jit(solution)/shard_map/all_gather | solution.py:44
  71.0 34.4 %copy-start.8 = (s32[4]{0:T(128)S(1)}, s32[4]{0:T(128)}, u32[]{:S(2)}) copy-start(s32[4]{0:T(128)} %param.14) | copy-start | bytes 52
  71.0 35.1 %copy-start.6 = (s32[4]{0:T(128)S(1)}, s32[4]{0:T(128)}, u32[]{:S(2)}) copy-start(s32[4]{0:T(128)} %param.15) | copy-start | bytes 52
  71.0 35.4 %copy-start.9 = (u32[32]{0:T(128)S(1)}, u32[32]{0:T(128)}, u32[]{:S(2)}) copy-start(u32[32]{0:T(128)} %constant.61) | copy-start | bytes 388
  71.1 51.7 %copy-start.5 = (s32[512]{0:T(512)S(1)}, s32[512]{0:T(512)}, u32[]{:S(2)}) copy-start(s32[512]{0:T(512)} %param.13) | copy-start | bytes 6148
  71.1 53.1 %copy-start.1 = (bf16[512,1280]{1,0:T(8,128)(2,1)S(1)}, bf16[512,1280]{1,0:T(8,128)(2,1)}, u32[]{:S(2)}) copy-start(bf16[512,1280]{1,0:T(8,128)(2,1)} %param.8) | copy-start | bytes 3932164
  71.1 65.2 %copy-start.7 = (f32[1280]{0:T(1024)S(1)}, f32[1280]{0:T(1024)}, u32[]{:S(2)}) copy-start(f32[1280]{0:T(1024)} %param.9) | copy-start | bytes 15364
  71.1 99.9 %all-gather.9.cloned.1.call-start = ((), (), s32[]{:S(2)}) async-start(), calls=%async_computation.4 | async-start | bytes 4096000 | tf_op jit(solution)/shard_map/all_gather | solution.py:74
  118.2 60.2 %all-to-all-start = ((s32[16,8,1]{0,2,1:T(1,128)}), s32[16,8,1]{0,2,1:T(1,128)S(1)}, u32[]{:S(2)}, u32[]{:S(2)}) async-start(s32[16,8,1]{0,2,1:T(1,128)} %copy.39), calls=%async_computation | async-start | bytes 8192 | tf_op jit(solution)/shard_map/all_to_all | solution.py:103
  163.6 1.6 copy-start
  167.8 3.3 %copy-start.2 = (bf16[512,1280]{1,0:T(8,128)(2,1)S(1)}, bf16[512,1280]{1,0:T(8,128)(2,1)}, u32[]{:S(2)}) copy-start(bf16[512,1280]{1,0:T(8,128)(2,1)} %param.8) | copy-start | bytes 3932164
  171.1 4.4 %copy-start.4 = (f32[1280]{0:T(1024)S(1)}, f32[1280]{0:T(1024)}, u32[]{:S(2)}) copy-start(f32[1280]{0:T(1024)} %param.12) | copy-start | bytes 15364
  178.3 37.3 %all-to-all-start.1 = ((bf16[16,8,5120]{2,0,1:T(8,128)(2,1)}), bf16[16,8,5120]{2,0,1:T(8,128)(2,1)S(1)}, u32[]{:S(2)}, u32[]{:S(2)}) async-start(bf16[16,8,5120]{2,0,1:T(8,128)(2,1)} %copy.47), calls=%async_computation.1 | async-start | bytes 2621440 | tf_op jit(solution)/shard_map/all_to_all | solution.py:102
Sparse Core Ops, SparseCore 0:
  9.5 57.1 all-gather.4
  71.2 65.0 all-gather.6
  137.8 29.2 all-gather.8
where the time goes:
time: 224 us
  waiting for transfers between devices  103 us (46%)
  blocking collectives  41.6 us (19%)
  local copies, waits for them, and re-layouts  29.9 us (13%)
  matrix products  19.4 us (9%)
  between operations  14 us (6%)
  starting transfers between devices  10.1 us (5%)
  other arithmetic  5.32 us (2%)
    all_gather x1, waiting for transfers between devices, body(): qkv_rows = lax.all_gather(w_qkv, 'tensor', axis=0, tiled=True)  59.4 us
    all_gather x1, blocking collectives, body(): proj_rows = lax.all_gather(w_out, 'tensor', axis=0, tiled=True)  33 us
    all_to_all x1, waiting for transfers between devices, body(): lax.all_to_all(outgoing, 'tensor', split_axis=1, concat_axis=0, tiled=True)  31.7 us
    reshape x3, local copies, waits for them, and re-layouts, split_heads(): return block.reshape(tile_count, WINDOW, HEADS, head_width)  13.2 us
    all_gather x1, waiting for transfers between devices, body(): lax.all_gather(qkv_rows, 'pipe', axis=1, tiled=True)  11.6 us
    dot_general x1, matrix products, body(): jnp.dot(normed, lax.all_gather(qkv_rows, 'pipe', axis=1, tiled=True), pre...  9.49 us
    unnamed x1, blocking collectives  8.57 us
    all_to_all x1, starting transfers between devices, body(): lax.all_to_all(outgoing, 'tensor', split_axis=1, concat_axis=0, tiled=True)  5.51 us
  transfers between devices with their start and end apart: 5, of which 3 were waited for; matrix products, arithmetic and copies ran while one was open for 22% of the time, Pallas kernels for 0%

commit v1 on v0

--- a/solution.py
+++ b/solution.py
@@ -1,8 +1,11 @@
+import functools
 import math
 
 import jax
 import jax.numpy as jnp
 from jax import lax
+from jax.experimental import pallas as pl
+from jax.experimental.pallas import tpu as pltpu
 from jax.sharding import PartitionSpec as P
 
 HEADS = 16
@@ -114,9 +117,375 @@
     return placed.astype(jnp.bfloat16).reshape(1, token_count, 1, 4 * feature_width)
 
 
+CORES = 2
+CHIPS_X = 2
+MESH = pl.DeviceIdType.MESH
+
+
+def kernel(
+    lines, group, x_ref, gain_ref, wq_in, wo_in, mgain_ref, wid_ref, count_ref, sample_ref, out_ref,
+    wq, wo, xp, normed, qkv, bias, hid, merged, recv, meta, msend,
+    own_sem, ss, rs, a_send, a_recv, a_own, m_send, m_recv,
+):
+    pipe, tens = lax.axis_index("pipe"), lax.axis_index("tensor")
+    y, c = pipe // CORES, pipe % CORES
+    z, x = tens // CHIPS_X, tens % CHIPS_X
+    weights = (wq, wo)
+    features = x_ref.shape[1]
+    blocks = x_ref.shape[0] // 128
+    width = features // HEADS
+    per_dest = 128 // group
+
+    def slot(w, y_, z_, x_, half=None, core=c):
+        rows = (wq_in, wo_in)[w].shape[0]
+        start = (z_ * CHIPS_X + x_) * rows
+        if half is not None:
+            rows = rows // 2
+            start = start + half * rows
+        return weights[w].at[y_ * CORES + core, pl.ds(pl.multiple_of(start, 16), rows)]
+
+    def copy(ref, send, receive, device):
+        return pltpu.make_async_remote_copy(
+            src_ref=ref, dst_ref=ref, send_sem=send, recv_sem=receive,
+            device_id=device, device_id_type=MESH,
+        )
+
+    to_x = {"tensor": z * CHIPS_X + 1 - x}
+    to_y = {"pipe": (1 - y) * CORES + c}
+    to_core = {"pipe": y * CORES + 1 - c}
+    to_up = {"tensor": (z + 1) * CHIPS_X + x}
+    to_down = {"tensor": (z - 1) * CHIPS_X + x}
+
+    def up(w, z_):
+        return copy(slot(w, y, z_, x), ss.at[w, 0, z_], rs.at[w, 0, z_], to_up)
+
+    def down(w, z_):
+        return copy(slot(w, y, z_, x), ss.at[w, 1, z_], rs.at[w, 0, z_], to_down)
+
+    names = ("x", "y", "xy", "yx", "c0", "cx", "cy", "cd")
+
+    def other(w, z_, name):
+        return {
+            "x": lambda: copy(slot(w, y, z_, x), ss.at[w, 2, z_], rs.at[w, 1, z_], to_x),
+            "y": lambda: copy(slot(w, y, z_, x), ss.at[w, 3, z_], rs.at[w, 2, z_], to_y),
+            "xy": lambda: copy(slot(w, y, z_, 1 - x, 0), ss.at[w, 4, z_], rs.at[w, 3, z_], to_y),
+            "yx": lambda: copy(slot(w, 1 - y, z_, x, 1), ss.at[w, 5, z_], rs.at[w, 4, z_], to_x),
+            "c0": lambda: copy(slot(w, y, z_, x), ss.at[w, 6, z_], rs.at[w, 5, z_], to_core),
+            "cx": lambda: copy(slot(w, y, z_, 1 - x), ss.at[w, 7, z_], rs.at[w, 6, z_], to_core),
+            "cy": lambda: copy(slot(w, 1 - y, z_, x), ss.at[w, 8, z_], rs.at[w, 7, z_], to_core),
+            "cd": lambda: copy(slot(w, 1 - y, z_, 1 - x), ss.at[w, 9, z_], rs.at[w, 8, z_], to_core),
+        }[name]()
+
+    def arrived(w, kind, z_, ref):
+        copy(ref, ss.at[w, 0, z_], rs.at[w, kind, z_], to_x).wait_recv()
+
+    def line_step(w, z_, own=False):
+        if not own:
+            arrived(w, 0, z_, slot(w, y, z_, x))
+
+        @pl.when((z_ <= z) & (z < lines - 1))
+        def _():
+            up(w, z_).start()
+
+        @pl.when((z_ >= z) & (z > 0))
+        def _():
+            down(w, z_).start()
+
+        for name in ("x", "y", "c0"):
+            other(w, z_, name).start()
+
+    def plane_step(w, z_):
+        arrived(w, 1, z_, slot(w, y, z_, 1 - x))
+        other(w, z_, "xy").start()
+        other(w, z_, "cx").start()
+        arrived(w, 2, z_, slot(w, 1 - y, z_, x))
+        other(w, z_, "yx").start()
+        other(w, z_, "cy").start()
+
+    def corner_step(w, z_):
+        arrived(w, 3, z_, slot(w, 1 - y, z_, 1 - x, 0))
+        arrived(w, 4, z_, slot(w, 1 - y, z_, 1 - x, 1))
+        other(w, z_, "cd").start()
+
+    offsets = [0]
+    for far in range(1, lines):
+        offsets += [-far, far]
+
+    def when_valid(offset, fn, w):
+        z_ = z + offset
+
+        @pl.when((z_ >= 0) & (z_ < lines))
+        def _():
+            fn(w, z_)
+
+    def gather_steps(w):
+        steps = []
+        for i in range(len(offsets) + 2):
+            def step(i=i):
+                if 0 < i < len(offsets):
+                    when_valid(offsets[i], line_step, w)
+                if 0 <= i - 1 < len(offsets):
+                    when_valid(offsets[i - 1], plane_step, w)
+                if 0 <= i - 2 < len(offsets):
+                    when_valid(offsets[i - 2], corner_step, w)
+            steps.append(step)
+        return steps
+
+    owns = [
+        pltpu.make_async_copy(src, slot(w, y, z, x), own_sem.at[w])
+        for w, src in enumerate((wq_in, wo_in))
+    ]
+    for own in owns:
+        own.start()
+
+    block_sample = []
+    for block in range(blocks):
+        offset = jnp.int32(0)
+        value = jnp.int32(SAMPLES)
+        for image in range(count_ref.shape[0]):
+            units = count_ref[image] // 128
+            inside = jnp.where(block >= offset, 1, 0) * jnp.where(block < offset + units, 1, 0)
+            value = value + inside * (sample_ref[image] - SAMPLES)
+            offset = offset + units
+        block_sample.append(value)
+    columns = group * blocks * per_dest
+    lane_block = (lax.broadcasted_iota(jnp.int32, (8, columns), 1) // per_dest) % blocks
+    own_meta = jnp.zeros((8, columns), jnp.int32)
+    for block in range(blocks):
+        own_meta = own_meta + jnp.where(lane_block == block, block_sample[block], 0)
+    msend[...] = own_meta
+
+    for w in (0, 1):
+        owns[w].wait()
+        line_step(w, z, own=True)
+
+    to_row = lax.broadcasted_iota(jnp.int32, (128, 128), 0)
+    from_row = lax.broadcasted_iota(jnp.int32, (128, 128), 1)
+    source = (to_row % per_dest // 4) * (4 * group) + (to_row // per_dest) * 4 + to_row % 4
+    permute = jnp.where(from_row == source, 1.0, 0.0).astype(jnp.bfloat16)
+    wid = wid_ref[...].astype(jnp.float32).astype(jnp.bfloat16)
+    across = (((1,), (1,)), ((), ()))
+    wid_lane = lax.dot_general(wid, permute, across, preferred_element_type=jnp.float32)
+    wid_row = lax.dot_general(permute, wid, across, preferred_element_type=jnp.float32)
+    for block in range(blocks):
+        same = wid_row[:, block : block + 1] == wid_lane[block : block + 1, :]
+        bias[block] = jnp.where(same, 0.0, -1e30)
+
+    def norm_block(block, carry):
+        rows = pl.ds(pl.multiple_of(block * 128, 128), 128)
+        moved = jnp.dot(permute, x_ref[rows, :], preferred_element_type=jnp.float32)
+        xp[rows, :] = moved.astype(jnp.bfloat16)
+        scale = lax.rsqrt(jnp.mean(moved * moved, axis=-1, keepdims=True) + epsilon)
+        normed[rows, :] = (moved * scale * gain_ref[...]).astype(jnp.bfloat16)
+        return carry
+
+    lax.fori_loop(0, blocks, norm_block, 0)
+
+    def meta_copy(m):
+        peer = lax.rem(tens + m, group)
+        return pltpu.make_async_remote_copy(
+            src_ref=msend, dst_ref=meta.at[tens], send_sem=m_send.at[m - 1],
+            recv_sem=m_recv.at[m - 1], device_id={"tensor": peer}, device_id_type=MESH,
+        )
+
+    for m in range(1, group):
+        meta_copy(m).start()
+    meta[tens] = own_meta
+
+    for step in gather_steps(0):
+        step()
+
+    late = gather_steps(1)
+
+    def core_arrived(w):
+        for z_ in range(lines):
+            arrived(w, 5, z_, slot(w, y, z_, x, core=1 - c))
+            arrived(w, 6, z_, slot(w, y, z_, 1 - x, core=1 - c))
+            arrived(w, 7, z_, slot(w, 1 - y, z_, x, core=1 - c))
+            arrived(w, 8, z_, slot(w, 1 - y, z_, 1 - x, core=1 - c))
+
+    core_arrived(0)
+    part = wq_in.shape[1]
+    for p in range(wq.shape[0]):
+        for first in range(0, part, 256):
+            last = min(first + 256, part)
+            product = jnp.dot(
+                normed[...], wq[p, :, first:last], preferred_element_type=jnp.float32
+            )
+            qkv[:, p * part + first : p * part + last] = product.astype(jnp.bfloat16)
+            if late:
+                late.pop(0)()
+    while late:
+        late.pop(0)()
+    core_arrived(1)
+
+    def exchange(block, m):
+        peer = lax.rem(tens + m, group)
+        return pltpu.make_async_remote_copy(
+            src_ref=merged.at[block, pl.ds(pl.multiple_of(peer * per_dest, per_dest), per_dest)],
+            dst_ref=recv.at[pl.ds(pl.multiple_of((tens * blocks + block) * per_dest, per_dest), per_dest)],
+            send_sem=a_send.at[block, m - 1],
+            recv_sem=a_recv.at[block, m - 1],
+            device_id={"tensor": peer},
+            device_id_type=MESH,
+        )
+
+    def keep(block):
+        return pltpu.make_async_copy(
+            merged.at[block, pl.ds(pl.multiple_of(tens * per_dest, per_dest), per_dest)],
+            recv.at[pl.ds(pl.multiple_of((tens * blocks + block) * per_dest, per_dest), per_dest)],
+            a_own.at[block],
+        )
+
+    out_part = wo_in.shape[1]
+
+    def attend(block, carry):
+        rows = pl.ds(pl.multiple_of(block * 128, 128), 128)
+        pieces = [None] * (features // 128)
+        mask = bias[block]
+        for head in range(HEADS):
+            low, high = head * width, (head + 1) * width
+            g0, g1 = low // 128, (high - 1) // 128 + 1
+            lanes = lax.broadcasted_iota(jnp.int32, (128, (g1 - g0) * 128), 1) + g0 * 128
+            in_head = (lanes >= low) & (lanes < high)
+            query = qkv[rows, g0 * 128 : g1 * 128]
+            key = qkv[rows, features + g0 * 128 : features + g1 * 128]
+            value = qkv[rows, 2 * features + g0 * 128 : 2 * features + g1 * 128]
+            query = jnp.where(in_head, query, jnp.zeros_like(query))
+            score = lax.dot_general(query, key, across, preferred_element_type=jnp.float32)
+            score = score * (1.0 / math.sqrt(width)) + mask
+            weight = jnp.exp(score - jnp.max(score, axis=-1, keepdims=True))
+            total = jnp.sum(weight, axis=-1, keepdims=True)
+            mixed = jnp.dot(
+                weight.astype(jnp.bfloat16), value, preferred_element_type=jnp.float32
+            ) * (1.0 / total)
+            for g in range(g0, g1):
+                cut = slice((g - g0) * 128, (g - g0 + 1) * 128)
+                piece = mixed[:, cut]
+                if pieces[g] is not None:
+                    piece = jnp.where(in_head[:, cut], piece, pieces[g])
+                pieces[g] = piece
+        live = jnp.float32(0)
+        for other in range(blocks):
+            alive = jnp.where(block_sample[other] < SAMPLES, 1.0, 0.0)
+            live = live + jnp.where(block == other, alive, 0.0)
+        context = (jnp.concatenate(pieces, axis=1) * live).astype(jnp.bfloat16)
+        for p in range(wo.shape[0]):
+            hid[:, p * out_part : (p + 1) * out_part] = jnp.dot(
+                context, wo[p], preferred_element_type=jnp.float32
+            )
+        hidden = hid[...] + xp[rows, :].astype(jnp.float32)
+        scale = lax.rsqrt(jnp.mean(hidden * hidden, axis=-1, keepdims=True) + epsilon)
+        merged[block] = (hidden * scale * mgain_ref[...]).astype(jnp.bfloat16)
+        for m in range(1, group):
+            exchange(block, m).start()
+        keep(block).start()
+        return carry
+
+    lax.fori_loop(0, blocks, attend, 0)
+
+    for m in range(1, group):
+        meta_copy(m).wait()
+    lane = lax.broadcasted_iota(jnp.int32, (1, columns), 1)
+    sample_lane = jnp.zeros((1, columns), jnp.int32)
+    for source_rank in range(group):
+        sample_lane = sample_lane + jnp.where(
+            lane // (blocks * per_dest) == source_rank, meta[source_rank, 0:1, :], 0
+        )
+    order = (sample_lane * columns + lane).astype(jnp.float32)
+    order_down = jnp.transpose(jnp.broadcast_to(order, (128, columns)))
+    ranks = []
+    for first in range(0, columns, 128):
+        before = jnp.where(order_down < order[:, first : first + 128], 1.0, 0.0)
+        ranks.append(jnp.sum(before, axis=0, keepdims=True))
+    rank = jnp.concatenate(ranks, axis=1)
+    rank = jnp.where(sample_lane < SAMPLES, rank, -1.0)
+
+    def drain(block, carry):
+        for m in range(1, group):
+            exchange(block, m).wait()
+        keep(block).wait()
+        return carry
+
+    lax.fori_loop(0, blocks, drain, 0)
+
+    tokens = out_ref.shape[0]
+    target = (lax.broadcasted_iota(jnp.int32, (tokens, columns), 0) * 4).astype(jnp.float32)
+    for k in range(4):
+        place = jnp.where(rank == target + k, 1.0, 0.0).astype(jnp.bfloat16)
+        placed = jnp.dot(place, recv[...], preferred_element_type=jnp.float32)
+        out_ref[:, k * features : (k + 1) * features] = placed.astype(jnp.bfloat16)
+
+    for w in (0, 1):
+        for z_ in range(lines):
+            for name in names:
+                other(w, z_, name).wait_send()
+
+            @pl.when((z_ <= z) & (z < lines - 1))
+            def _():
+                up(w, z_).wait_send()
+
+            @pl.when((z_ >= z) & (z > 0))
+            def _():
+                down(w, z_).wait_send()
+
+
+def fused_body(pipe, group, patches, attn_gain, w_qkv, w_out, merge_gain, window_ids, image_patches, image_sample):
+    slots, features = patches.shape
+    blocks = slots // 128
+    lines = group // CHIPS_X
+    columns = group * blocks * (128 // group)
+    bf16, f32, i32 = jnp.bfloat16, jnp.float32, jnp.int32
+    vmem = pl.BlockSpec(memory_space=pltpu.VMEM)
+    smem = pl.BlockSpec(memory_space=pltpu.SMEM)
+    hbm = pl.BlockSpec(memory_space=pl.ANY)
+    dma = pltpu.SemaphoreType.DMA
+    placed = pl.pallas_call(
+        functools.partial(kernel, lines, group),
+        out_shape=jax.ShapeDtypeStruct((slots // 4, 4 * features), bf16),
+        in_specs=[vmem, vmem, hbm, hbm, vmem, vmem, smem, smem],
+        out_specs=vmem,
+        scratch_shapes=[
+            pltpu.VMEM((pipe, w_qkv.shape[0] * group, w_qkv.shape[1]), bf16),
+            pltpu.VMEM((pipe, w_out.shape[0] * group, w_out.shape[1]), bf16),
+            pltpu.VMEM((slots, features), bf16),
+            pltpu.VMEM((slots, features), bf16),
+            pltpu.VMEM((slots, 3 * features), bf16),
+            pltpu.VMEM((blocks, 128, 128), f32),
+            pltpu.VMEM((128, features), f32),
+            pltpu.VMEM((blocks, 128, features), bf16),
+            pltpu.VMEM((slots, features), bf16),
+            pltpu.VMEM((group, 8, columns), i32),
+            pltpu.VMEM((8, columns), i32),
+            dma((2,)),
+            dma((2, 10, lines)),
+            dma((2, 9, lines)),
+            dma((blocks, group - 1)),
+            dma((blocks, group - 1)),
+            dma((blocks,)),
+            dma((group - 1,)),
+            dma((group - 1,)),
+        ],
+        compiler_params=pltpu.CompilerParams(
+            has_side_effects=True, vmem_limit_bytes=60 * 1024 * 1024
+        ),
+    )(
+        patches, attn_gain[None, :], w_qkv, w_out, merge_gain[None, :],
+        window_ids.reshape(blocks, 128), image_patches, image_sample,
+    )
+    return placed.reshape(1, slots // 4, 1, 4 * features)
+
+
+def fits(mesh):
+    return mesh.shape["pipe"] == 2 * CORES and mesh.shape["tensor"] == 8
+
+
 def solution(mesh):
+    chosen = body
+    if fits(mesh):
+        chosen = functools.partial(fused_body, mesh.shape["pipe"], mesh.shape["tensor"])
     return jax.shard_map(
-        body,
+        chosen,
         mesh=mesh,
         in_specs=(
             P(("pipe", "tensor"), None),

time: 224 us -> 125 us (0.56)
  Pallas kernels: 0 us -> 120 us
  waiting for transfers between devices: 103 us -> 0 us
  blocking collectives: 41.6 us -> 0 us
  local copies, waits for them, and re-layouts: 29.9 us -> 5.04 us
  matrix products: 19.4 us -> 0 us
  between operations: 14 us -> 0.01 us
  starting transfers between devices: 10.1 us -> 0 us
  other arithmetic: 5.32 us -> 0 us
    pallas_call x0 -> x1, Pallas kernels: none -> 120 us  [fused_body(): pl.pallas_call(functools.partial(kernel, lines, group), out_shape=jax.Sha...]
    all_gather x3 -> x0, waiting for transfers between devices: 71 us -> none  [the longest x1 59.4 us: body(): qkv_rows = lax.all_gather(w_qkv, 'tensor', axis=0, tiled=True)]
    all_gather x1 -> x0, blocking collectives: 33 us -> none  [body(): proj_rows = lax.all_gather(w_out, 'tensor', axis=0, tiled=True)]
    all_to_all x2 -> x0, waiting for transfers between devices: 31.7 us -> none  [the longest x1 31.7 us: body(): lax.all_to_all(outgoing, 'tensor', split_axis=1, concat_axis=0, tiled=True)]
    dot_general x5 -> x0, matrix products: 19.4 us -> none  [the longest x1 9.49 us: body(): jnp.dot(normed, lax.all_gather(qkv_rows, 'pipe', axis=1, tiled=True), pre...]
    reshape x5 -> x0, local copies, waits for them, and re-layouts: 16.6 us -> none  [the longest x3 13.2 us: split_heads(): return block.reshape(tile_count, WINDOW, HEADS, head_width)]
    all_to_all x2 -> x0, starting transfers between devices: 10 us -> none  [the longest x1 5.51 us: body(): lax.all_to_all(outgoing, 'tensor', split_axis=1, concat_axis=0, tiled=True)]
    unnamed x1 -> x0, blocking collectives: 8.57 us -> none
  transfers between devices with their start and end apart: 5 -> 0, of which waited for: 3 -> 0; matrix products, arithmetic and copies ran while one was open for 22% -> 0% of each run, Pallas kernels for 0% -> 0%
where the time goes in v1:
time: 125 us
  Pallas kernels  120 us (96%)
  local copies, waits for them, and re-layouts  5.04 us (4%)
    pallas_call x1, Pallas kernels, fused_body(): pl.pallas_call(functools.partial(kernel, lines, group), out_shape=jax.Sha...  120 us

profile of v1, /device:TPU:0, one launch (start us, length us, event | category | flops | bytes accessed | tf_op | source)
XLA Modules:
  0.0 124.8 jit_solution(7088271600282631886)
XLA Ops:
  0.0 1.3 %broadcast_in_dim.6.gain_ref = f32[1,1280]{1,0:T(1,128)} reshape(f32[1280]{0:T(1024)} %param.9) | data formatting | bytes 10240 | tf_op jit(solution)/shard_map/broadcast_in_dim | solution.py:473
  1.3 1.3 %broadcast_in_dim.7.mgain_ref = f32[1,1280]{1,0:T(1,128)} reshape(f32[1280]{0:T(1024)} %param.12) | data formatting | bytes 10240 | tf_op jit(solution)/shard_map/broadcast_in_dim | solution.py:473
  2.6 119.8 %shard_map.82 = bf16[128,5120]{1,0:T(8,128)(2,1)} custom-call(bf16[512,1280]{1,0:T(8,128)(2,1)} %x_ref.1, f32[1,1280]{1,0:T(1,128)} %broadcast_in_dim.6.gain_ref, bf16[160,960]{1,0:T(8,128)(2,1)} %wq_in.1, bf16[160,320]{1,0:T(8,128)(2,1)} %wo_in.1, f32[1,1280]{1,0:T(1,128)} %broadcast_in_dim.7.mgain_ref, s32[4,128]{1,0:T(4,128)} %bitcast.3, s32[4]{0:T(128)} %count_ref.1, ...), custom_call_target="tpu_custom_call" | custom-call | tf_op jit(solution)/shard_map/pallas_call | solution.py:443
  122.4 2.5 %copy.10 = bf16[1,128,1,5120]{3,1,2,0:T(8,128)(2,1)} copy(bf16[1,128,1,5120]{3,1,2,0:T(8,128)(2,1)} %bitcast.2) | data formatting | bytes 2621440

commit v2 on v1

--- a/solution.py
+++ b/solution.py
@@ -124,7 +124,7 @@
 
 def kernel(
     lines, group, x_ref, gain_ref, wq_in, wo_in, mgain_ref, wid_ref, count_ref, sample_ref, out_ref,
-    wq, wo, xp, normed, qkv, bias, hid, merged, recv, meta, msend,
+    wq, wo, xp, normed, qkv, context, bias, hid, merged, recv, meta, msend,
     own_sem, ss, rs, a_send, a_recv, a_own, m_send, m_recv,
 ):
     pipe, tens = lax.axis_index("pipe"), lax.axis_index("tensor")
@@ -217,19 +217,6 @@
         @pl.when((z_ >= 0) & (z_ < lines))
         def _():
             fn(w, z_)
-
-    def gather_steps(w):
-        steps = []
-        for i in range(len(offsets) + 2):
-            def step(i=i):
-                if 0 < i < len(offsets):
-                    when_valid(offsets[i], line_step, w)
-                if 0 <= i - 1 < len(offsets):
-                    when_valid(offsets[i - 1], plane_step, w)
-                if 0 <= i - 2 < len(offsets):
-                    when_valid(offsets[i - 2], corner_step, w)
-            steps.append(step)
-        return steps
 
     owns = [
         pltpu.make_async_copy(src, slot(w, y, z, x), own_sem.at[w])
@@ -292,32 +279,47 @@
         meta_copy(m).start()
     meta[tens] = own_meta
 
-    for step in gather_steps(0):
-        step()
-
-    late = gather_steps(1)
-
-    def core_arrived(w):
+    lag = 3
+    for i in range(len(offsets) + lag):
+        if 0 < i < len(offsets):
+            when_valid(offsets[i], line_step, 0)
+        if i >= lag:
+            when_valid(offsets[i - lag], plane_step, 0)
+    for offset in offsets[1:]:
+        when_valid(offset, line_step, 1)
+
+    def core_arrived(w, own_plane):
         for z_ in range(lines):
-            arrived(w, 5, z_, slot(w, y, z_, x, core=1 - c))
-            arrived(w, 6, z_, slot(w, y, z_, 1 - x, core=1 - c))
-            arrived(w, 7, z_, slot(w, 1 - y, z_, x, core=1 - c))
-            arrived(w, 8, z_, slot(w, 1 - y, z_, 1 - x, core=1 - c))
-
-    core_arrived(0)
+            if own_plane:
+                arrived(w, 5, z_, slot(w, y, z_, x, core=1 - c))
+                arrived(w, 6, z_, slot(w, y, z_, 1 - x, core=1 - c))
+            else:
+                arrived(w, 7, z_, slot(w, 1 - y, z_, x, core=1 - c))
+                arrived(w, 8, z_, slot(w, 1 - y, z_, 1 - x, core=1 - c))
+
     part = wq_in.shape[1]
-    for p in range(wq.shape[0]):
-        for first in range(0, part, 256):
-            last = min(first + 256, part)
-            product = jnp.dot(
-                normed[...], wq[p, :, first:last], preferred_element_type=jnp.float32
-            )
-            qkv[:, p * part + first : p * part + last] = product.astype(jnp.bfloat16)
-            if late:
-                late.pop(0)()
-    while late:
-        late.pop(0)()
-    core_arrived(1)
+
+    def project(plane, between):
+        for core in range(CORES):
+            for first in range(0, part, 256):
+                last = min(first + 256, part)
+                product = jnp.dot(
+                    normed[...],
+                    wq[plane * CORES + core, :, first:last],
+                    preferred_element_type=jnp.float32,
+                )
+                qkv[plane, :, core * part + first : core * part + last] = product.astype(jnp.bfloat16)
+                if between:
+                    between.pop(0)()
+
+    core_arrived(0, True)
+    project(y, [])
+    for offset in offsets:
+        when_valid(offset, corner_step, 0)
+    core_arrived(0, False)
+    project(
+        1 - y, [functools.partial(when_valid, offset, plane_step, 1) for offset in offsets]
+    )
 
     def exchange(block, m):
         peer = lax.rem(tens + m, group)
@@ -338,6 +340,13 @@
         )
 
     out_part = wo_in.shape[1]
+    ahead = min(2, blocks)
+
+    half = qkv.shape[2]
+
+    def lanes_of(rows, start, stop):
+        plane = start // half
+        return qkv[plane, rows, start - plane * half : stop - plane * half]
 
     def attend(block, carry):
         rows = pl.ds(pl.multiple_of(block * 128, 128), 128)
@@ -348,9 +357,9 @@
             g0, g1 = low // 128, (high - 1) // 128 + 1
             lanes = lax.broadcasted_iota(jnp.int32, (128, (g1 - g0) * 128), 1) + g0 * 128
             in_head = (lanes >= low) & (lanes < high)
-            query = qkv[rows, g0 * 128 : g1 * 128]
-            key = qkv[rows, features + g0 * 128 : features + g1 * 128]
-            value = qkv[rows, 2 * features + g0 * 128 : 2 * features + g1 * 128]
+            query, key, value = (
+                lanes_of(rows, i * features + g0 * 128, i * features + g1 * 128) for i in range(3)
+            )
             query = jnp.where(in_head, query, jnp.zeros_like(query))
             score = lax.dot_general(query, key, across, preferred_element_type=jnp.float32)
             score = score * (1.0 / math.sqrt(width)) + mask
@@ -366,13 +375,18 @@
                     piece = jnp.where(in_head[:, cut], piece, pieces[g])
                 pieces[g] = piece
         live = jnp.float32(0)
-        for other in range(blocks):
-            alive = jnp.where(block_sample[other] < SAMPLES, 1.0, 0.0)
-            live = live + jnp.where(block == other, alive, 0.0)
-        context = (jnp.concatenate(pieces, axis=1) * live).astype(jnp.bfloat16)
+        for other_block in range(blocks):
+            alive = jnp.where(block_sample[other_block] < SAMPLES, 1.0, 0.0)
+            live = live + jnp.where(block == other_block, alive, 0.0)
+        for g, piece in enumerate(pieces):
+            context[rows, g * 128 : (g + 1) * 128] = (piece * live).astype(jnp.bfloat16)
+        return carry
+
+    def finish(block, carry):
+        rows = pl.ds(pl.multiple_of(block * 128, 128), 128)
         for p in range(wo.shape[0]):
             hid[:, p * out_part : (p + 1) * out_part] = jnp.dot(
-                context, wo[p], preferred_element_type=jnp.float32
+                context[rows, :], wo[p], preferred_element_type=jnp.float32
             )
         hidden = hid[...] + xp[rows, :].astype(jnp.float32)
         scale = lax.rsqrt(jnp.mean(hidden * hidden, axis=-1, keepdims=True) + epsilon)
@@ -382,7 +396,22 @@
         keep(block).start()
         return carry
 
-    lax.fori_loop(0, blocks, attend, 0)
+    lax.fori_loop(0, ahead, attend, 0)
+    for offset in offsets:
+        when_valid(offset, corner_step, 1)
+    core_arrived(1, True)
+    core_arrived(1, False)
+
+    def pair(block, carry):
+        finish(block, carry)
+
+        @pl.when(block + ahead < blocks)
+        def _():
+            attend(block + ahead, 0)
+
+        return carry
+
+    lax.fori_loop(0, blocks, pair, 0)
 
     for m in range(1, group):
         meta_copy(m).wait()
@@ -450,7 +479,8 @@
             pltpu.VMEM((pipe, w_out.shape[0] * group, w_out.shape[1]), bf16),
             pltpu.VMEM((slots, features), bf16),
             pltpu.VMEM((slots, features), bf16),
-            pltpu.VMEM((slots, 3 * features), bf16),
+            pltpu.VMEM((pipe // CORES, slots, CORES * w_qkv.shape[1]), bf16),
+            pltpu.VMEM((slots, features), bf16),
             pltpu.VMEM((blocks, 128, 128), f32),
             pltpu.VMEM((128, features), f32),
             pltpu.VMEM((blocks, 128, features), bf16),

time: 125 us -> 116 us (0.928)
  Pallas kernels: 120 us -> 110 us
    pallas_call x1, Pallas kernels: 120 us -> 110 us  [fused_body(): pl.pallas_call(functools.partial(kernel, lines, group), out_shape=jax.Sha...]
where the time goes in v2:
time: 116 us; the launch traced here: 115 us
  Pallas kernels  110 us (95%)
  local copies, waits for them, and re-layouts  5.04 us (4%)
    pallas_call x1, Pallas kernels, fused_body(): pl.pallas_call(functools.partial(kernel, lines, group), out_shape=jax.Sha...  110 us
    unnamed x1, local copies, waits for them, and re-layouts  2.46 us

profile of v2, /device:TPU:0, one launch (start us, length us, event | category | flops | bytes accessed | tf_op | source)
XLA Modules:
  0.0 114.7 jit_solution(16241733475242041796)
XLA Ops:
  0.0 1.3 %broadcast_in_dim.6.gain_ref = f32[1,1280]{1,0:T(1,128)} reshape(f32[1280]{0:T(1024)} %param.9) | data formatting | bytes 10240 | tf_op jit(solution)/shard_map/broadcast_in_dim | solution.py:503
  1.3 1.3 %broadcast_in_dim.7.mgain_ref = f32[1,1280]{1,0:T(1,128)} reshape(f32[1280]{0:T(1024)} %param.12) | data formatting | bytes 10240 | tf_op jit(solution)/shard_map/broadcast_in_dim | solution.py:503
  2.6 109.6 %shard_map.82 = bf16[128,5120]{1,0:T(8,128)(2,1)} custom-call(bf16[512,1280]{1,0:T(8,128)(2,1)} %x_ref.1, f32[1,1280]{1,0:T(1,128)} %broadcast_in_dim.6.gain_ref, bf16[160,960]{1,0:T(8,128)(2,1)} %wq_in.1, bf16[160,320]{1,0:T(8,128)(2,1)} %wo_in.1, f32[1,1280]{1,0:T(1,128)} %broadcast_in_dim.7.mgain_ref, s32[4,128]{1,0:T(4,128)} %bitcast.3, s32[4]{0:T(128)} %count_ref.1, ...), custom_call_target="tpu_custom_call" | custom-call | tf_op jit(solution)/shard_map/pallas_call | solution.py:472
  112.2 2.5 %copy.10 = bf16[1,128,1,5120]{3,1,2,0:T(8,128)(2,1)} copy(bf16[1,128,1,5120]{3,1,2,0:T(8,128)(2,1)} %bitcast.2) | data formatting | bytes 2621440
